TPU v7x, 32 devices: a whole 2x2x4 slice. The times are simulated.
32 devices in a mesh: outer: 8 (over y, x, core), span: 4 (over z).
Axes of the slice: x: 2, y: 2, z: 4, core: 2. Of those that a mesh axis runs over, the one named last changes fastest.
Arguments:
- queries_in: bfloat16 [16, 2048, 16, 128], P('outer', 'span'), may hold values from -6 to 6
- keys_in: bfloat16 [16, 2048, 16, 128], P('outer', 'span'), may hold values from -6 to 6
- values_in: bfloat16 [16, 2048, 16, 128], P('outer', 'span'), may hold values from -6 to 6
- gate_rows: bfloat16 [16, 2048, 16, 128], P('outer', 'span'), may hold values from -6 to 6
- out_weight: bfloat16 [2048, 2048], P('outer'), may hold values from -0.125 to 0.125
Outputs:
- mixer_out: bfloat16 [16, 2048, 2048], P('outer', 'span')
All inputs are finite; a program needn't handle non-finite values.
Results may differ from a plain program's by a relative error of at most 0.0023.
Values may be sent and summed in bfloat16 or wider, within the bound.
A program may use at most 256 MiB of HBM per device.

v0:
```python
import jax
import jax.numpy as jnp
from jax import lax
from jax.sharding import PartitionSpec as P


def taken_in(value, axis, dim, absorb, carry):
    whole = jax.tree.map(lambda part: lax.all_gather(part, axis, axis=dim, tiled=True), value)
    return absorb(carry, whole, jnp.int32(0))


def feature_map(values):
    wide = values.astype(jnp.float32)
    return jnp.where(wide > 0.0, wide + 1.0, jnp.exp(jnp.minimum(wide, 0.0))).astype(jnp.bfloat16)


def close_heads(read, gate_rows, count):
    result = read * count**0.5
    result = result * jax.nn.sigmoid(gate_rows.astype(jnp.float32))
    return result.astype(jnp.bfloat16)


def ask_state(features, state, mass):
    top = jnp.einsum(
        "bthd,bhde->bthe", features, state.astype(jnp.bfloat16), preferred_element_type=jnp.float32
    )
    bottom = jnp.einsum(
        "bthd,bhd->bth", features.astype(jnp.float32), mass, precision=lax.Precision.HIGHEST
    )
    return top / (bottom + 0.001)[..., None]


def body(queries_in, keys_in, values_in, gate_rows, out_weight):
    query_feature, key_feature = (feature_map(queries_in), feature_map(keys_in))
    count = queries_in.shape[1] * lax.axis_size("span")
    part_state = jnp.einsum(
        "bthd,bthe->bhde", key_feature, values_in, preferred_element_type=jnp.float32
    )
    part_mass = jnp.sum(key_feature.astype(jnp.float32), axis=1)
    state, mass = lax.psum((part_state, part_mass), "span")
    read = ask_state(query_feature, state / count, mass / count)
    mixed = close_heads(read, gate_rows, count)
    mixed = mixed.reshape(mixed.shape[0], mixed.shape[1], -1)

    def add_rows(carry, piece, start):
        part = lax.dynamic_slice_in_dim(mixed, start, piece.shape[0], axis=2)
        return carry + jnp.einsum("btw,wv->btv", part, piece, preferred_element_type=jnp.float32)

    blank = jnp.zeros(mixed.shape, jnp.float32)
    mixer_out = taken_in(out_weight, "outer", 0, add_rows, blank).astype(jnp.bfloat16)
    return mixer_out


def solution(mesh):
    in_specs = (
        P("outer", "span", None, None),
        P("outer", "span", None, None),
        P("outer", "span", None, None),
        P("outer", "span", None, None),
        P("outer", None),
    )
    out_specs = P("outer", "span", None)
    return jax.shard_map(body, mesh=mesh, in_specs=in_specs, out_specs=out_specs, check_vma=False)
```

profile of v0, /device:TPU:0, one launch (start us, length us, event | category | flops | bytes accessed | tf_op | source)
XLA Modules:
  0.0 142.2 jit_solution(3952385528680679636)
XLA Ops:
  7.4 0.0 all-reduce.2.cloned.1.call-start
  7.4 7.5 %copy.6 = bf16[2,512,16,128]{1,3,2,0:T(8,128)(2,1)} copy(bf16[2,512,16,128]{3,2,1,0:T(8,128)(2,1)} %param.6) | data formatting | bytes 8388608 | tf_op args[1]
  14.9 7.9 %fusion.11 = f32[2,16,128,128]{2,3,1,0:T(8,128)} fusion(bf16[2,512,16,128]{3,2,1,0:T(8,128)(2,1)} %param.7, bf16[2,512,16,128]{1,3,2,0:T(8,128)(2,1)} %copy.6), kind=kOutput, calls=%fused_computation.19 | convolution fusion | flops 549453824 | bytes 10485760 | tf_op jit(solution)/shard_map/bthd,bthe->bhde/dot_general | solution.py:36
  22.8 0.0 all-reduce.2.cloned.1.call-update
  22.8 0.0 all-gather.2.cloned.1.call-start
  22.9 0.5 all-gather.2.cloned.1.call-update
  23.4 7.5 %copy.7 = bf16[2,512,16,128]{1,3,2,0:T(8,128)(2,1)} copy(bf16[2,512,16,128]{3,2,1,0:T(8,128)(2,1)} %param.5) | data formatting | bytes 8388608 | tf_op args[0]
  30.9 7.5 %copy.9 = bf16[2,512,16,128]{1,3,2,0:T(8,128)(2,1)} copy(bf16[2,512,16,128]{3,2,1,0:T(8,128)(2,1)} %param.8) | data formatting | bytes 8388608 | tf_op args[3]
  38.4 3.9 %convert_reduce_fusion = f32[2,16,128]{2,1,0:T(8,128)S(1)} fusion(bf16[2,512,16,128]{1,3,2,0:T(8,128)(2,1)} %copy.6), kind=kLoop, calls=%fused_computation.18 | loop fusion | flops 16773120 | bytes 4210688 | tf_op jit(solution)/shard_map/reduce_sum | solution.py:39
  42.3 21.1 %psum.15 = f32[2,16,128]{2,1,0:T(8,128)S(1)} all-reduce(f32[2,16,128]{2,1,0:T(8,128)S(1)} %convert_reduce_fusion), channel_id=1, replica_groups=mesh['outer'=8,'span'=4] {'span'}, use_global_device_ids=true, to_apply=%region_2.3 | all-reduce | flops 4096 | bytes 32768 | tf_op jit(solution)/shard_map/psum | solution.py:40
  63.4 5.4 %fusion.17 = f32[2,16,1,512]{3,2,1,0:T(1,128)S(1)} fusion(f32[2,16,128,1]{2,3,1,0:T(1,128)S(1)} %bitcast.25, bf16[2,512,16,128]{1,3,2,0:T(8,128)(2,1)} %copy.7), kind=kOutput, calls=%fused_computation.23 | convolution fusion | flops 37748736 | bytes 4276224 | tf_op jit(solution)/shard_map/bthd,bhd->bth/dot_general | solution.py:27
  68.8 43.1 %all-reduce.2.cloned.1.call-done = f32[2,16,128,128]{2,3,1,0:T(8,128)} async-done(((f32[2,16,128,128]{2,3,1,0:T(8,128)}), f32[2,16,128,128]{2,3,1,0:T(8,128)}) %all-reduce.2.cloned.1.call-update) | async-done | bytes 2097168 | tf_op jit(solution)/shard_map/psum | solution.py:40
  111.9 8.9 %fusion.10 = bf16[2,512,16,128]{1,3,2,0:T(8,128)(2,1)} fusion(bf16[2,512,16,128]{1,3,2,0:T(8,128)(2,1)} %copy.9, f32[2,512,16]{1,2,0:T(8,128)S(1)} %fusion.21, bf16[2,512,16,128]{1,3,2,0:T(8,128)(2,1)} %copy.7, f32[2,16,128,128]{2,3,1,0:T(8,128)} %all-reduce.2.cloned.1.call-done), kind=kOutput, calls=%fused_computation.17 | convolution fusion | flops 567279616 | bytes 14745600 | tf_op jit(solution)/shard_map/bthd,bhde->bthe/dot_general | solution.py:24
  120.8 0.0 all-gather.2.cloned.1.call-done
  120.8 13.9 %fusion.13 = bf16[2,512,2048]{2,1,0:T(8,128)(2,1)} fusion(bf16[2,512,2048]{1,2,0:T(8,128)(2,1)} %bitcast.26, bf16[2048,2048]{1,0:T(8,128)(2,1)} %all-gather.2.cloned.1.call-done), kind=kOutput, calls=%fused_computation.21 | convolution fusion | flops 8592031744 | bytes 16777216 | tf_op jit(solution)/shard_map/btw,wv->btv/dot_general | solution.py:47
  (2 shorter events, 0.0 us)
Async XLA Ops:
  7.4 104.6 %all-reduce.2.cloned.1.call-start = ((), (), s32[]{:S(2)}) async-start(), calls=%async_computation | async-start | bytes 4194304 | tf_op jit(solution)/shard_map/psum | solution.py:40
  22.8 98.0 %all-gather.2.cloned.1.call-start = ((), (), s32[]{:S(2)}) async-start(), calls=%async_computation.1 | async-start | bytes 9437184 | tf_op jit(solution)/shard_map/all_gather | solution.py:8
Sparse Core Ops, SparseCore 0:
  22.9 88.9 all-reduce.1
Sparse Core Ops, SparseCore 1:
  25.2 56.7 all-gather.1
where the time goes:
time: 143 us; the launch traced here: 142 us
  waiting for transfers between devices  43.7 us (31%)
  matrix products  36.1 us (25%)
  local copies, waits for them, and re-layouts  22.5 us (16%)
  blocking collectives  21.1 us (15%)
  between operations  14.9 us (10%)
  other arithmetic  3.92 us (3%)
    psum x1, waiting for transfers between devices, body(): state, mass = lax.psum((part_state, part_mass), 'span')  43.1 us
    unnamed x3, local copies, waits for them, and re-layouts  22.5 us
    psum x1, blocking collectives, body(): state, mass = lax.psum((part_state, part_mass), 'span')  21.1 us
    dot_general x1, matrix products, add_rows(): jnp.einsum('btw,wv->btv', part, piece, preferred_element_type=jnp.float32)  13.9 us
    dot_general x1, matrix products, ask_state(): jnp.einsum('bthd,bhde->bthe', features, state.astype(jnp.bfloat16), prefe...  8.86 us
    dot_general x1, matrix products, body(): jnp.einsum('bthd,bthe->bhde', key_feature, values_in, preferred_element_t...  7.87 us
    dot_general x1, matrix products, ask_state(): jnp.einsum('bthd,bhd->bth', features.astype(jnp.float32), mass, precision...  5.43 us
    reduce_sum x1, other arithmetic, body(): part_mass = jnp.sum(key_feature.astype(jnp.float32), axis=1)  3.91 us
  transfers between devices with their start and end apart: 2, of which 1 were waited for; matrix products, arithmetic and copies ran while one was open for 23% of the time, Pallas kernels for 0%

commit v1 on v0

v1 whole, which is shorter than its diff:
```python
import functools

import jax
import jax.numpy as jnp
from jax import lax
from jax.experimental import pallas as pl
from jax.experimental.pallas import tpu as pltpu
from jax.sharding import PartitionSpec as P

MESH = pl.DeviceIdType.MESH
TILE = 64
ROWS = 128


def feature_map(values):
    wide = values.astype(jnp.float32)
    return jnp.where(wide > 0.0, wide + 1.0, jnp.exp(jnp.minimum(wide, 0.0))).astype(jnp.bfloat16)


def kernel(
    no, ns, q_hbm, k_hbm, v_hbm, g_hbm, w_hbm, mixed_hbm, wfull,
    kin, vin, qin, gin, wown, kf, vt, qf, gs, part, acc, rr, rl, sr, sl, full, mown, mrecv, mixed,
    in_sem, w_sem, out_sem, wsend, wrecv, rr_send, rr_recv, rl_send, rl_recv,
    ag_sr, ag_sl, ag_recv, m_send, m_recv,
):
    batch, tokens, heads, size = q_hbm.shape
    depth = w_hbm.shape[0]
    half = depth // 2
    chunk = heads // ns
    count = tokens * ns
    o = lax.axis_index("outer")
    s = lax.axis_index("span")

    def remote(src, dst, send, recv, **where):
        return pltpu.make_async_remote_copy(
            src_ref=src, dst_ref=dst, send_sem=send, recv_sem=recv, device_id=where, device_id_type=MESH
        )

    own_w = pltpu.make_async_copy(w_hbm, wown, w_sem.at[0])
    own_w.start()
    loads = {}
    for b in range(batch):
        for n, (src, dst) in enumerate(((k_hbm, kin), (v_hbm, vin))):
            loads[n, b] = pltpu.make_async_copy(src.at[b], dst.at[b], in_sem.at[n, b])
            loads[n, b].start()
    for b in range(batch):
        for n, (src, dst) in enumerate(((q_hbm, qin), (g_hbm, gin))):
            loads[n + 2, b] = pltpu.make_async_copy(src.at[b], dst.at[b], in_sem.at[n + 2, b])
            loads[n + 2, b].start()

    grid = no == 8
    dc, dx, dy = 1 - 2 * (o % 2), 2 - 4 * ((o // 2) % 2), 4 - 8 * ((o // 4) % 2)
    if grid:
        partners = [o + dc, o + dx, o + dy]
    else:
        partners = [(o + d) % no for d in range(1, no)]
    barrier = pltpu.get_barrier_semaphore()
    for other in partners:
        pl.semaphore_signal(barrier, inc=1, device_id={"outer": other}, device_id_type=MESH)
    for d in range(1, ns):
        pl.semaphore_signal(barrier, inc=1, device_id={"span": (s + d) % ns}, device_id_type=MESH)
    pl.semaphore_wait(barrier, len(partners) + ns - 1)

    def rows(block, part_of=None):
        if part_of is None:
            return wfull.at[pl.ds(pl.multiple_of(block * depth, depth), depth)]
        return wfull.at[pl.ds(pl.multiple_of(block * depth + part_of * half, half), half)]

    own_w.wait()
    keep_w = pltpu.make_async_copy(wown, rows(o), w_sem.at[1])
    keep_w.start()
    sends = []

    def w_copy(n, src, dst, other):
        copy = remote(src, dst, wsend.at[n], wrecv.at[n], outer=other)
        copy.start()
        sends.append(copy)

    def w_take(n, dst, other):
        remote(dst, dst, wsend.at[n], wrecv.at[n], outer=other).wait_recv()

    if grid:
        xn, yn, pn = o + dx, o + dy, o + dc
        for n, other, h in ((0, xn, 0), (3, yn, 1), (1, xn, 1), (2, yn, 0)):
            w_copy(n, wown.at[pl.ds(h * half, half)], rows(o, h), other)
        w_copy(6, wown, rows(o), pn)
    else:
        for d in range(1, no):
            w_copy(d, wown, rows(o), (o + d) % no)

    def weights_a():
        if grid:
            w_take(0, rows(xn, 0), xn)
            w_copy(4, rows(xn, 0), rows(xn, 0), yn)
            w_copy(7, rows(xn, 0), rows(xn, 0), pn)
            w_take(3, rows(yn, 1), yn)
            w_copy(5, rows(yn, 1), rows(yn, 1), xn)
            w_copy(8, rows(yn, 1), rows(yn, 1), pn)

    def weights_b():
        if grid:
            w_take(1, rows(xn, 1), xn)
            w_copy(9, rows(xn, 1), rows(xn, 1), pn)
            w_take(2, rows(yn, 0), yn)
            w_copy(10, rows(yn, 0), rows(yn, 0), pn)

    def weights_c():
        if grid:
            far = o + dx + dy
            w_take(4, rows(far, 0), yn)
            w_copy(11, rows(far, 0), rows(far, 0), pn)
            w_take(5, rows(far, 1), xn)
            w_copy(12, rows(far, 1), rows(far, 1), pn)
            w_take(6, rows(pn), pn)
            w_take(7, rows(pn + dx, 0), pn)
            w_take(8, rows(pn + dy, 1), pn)
            w_take(9, rows(pn + dx, 1), pn)
            w_take(10, rows(pn + dy, 0), pn)
            w_take(11, rows(pn + dx + dy, 0), pn)
            w_take(12, rows(pn + dx + dy, 1), pn)
        else:
            for d in range(1, no):
                w_take(d, rows((o + no - d) % no), (o + no - d) % no)

    def state(b):
        loads[0, b].wait()
        loads[1, b].wait()

        def turn(i, _):
            at = pl.ds(pl.multiple_of(i * TILE, TILE), TILE)
            kf[:, at, :] = jnp.swapaxes(feature_map(kin[b, at]), 0, 1)
            vt[:, at, :] = jnp.swapaxes(vin[b, at], 0, 1)
            return 0

        lax.fori_loop(0, tokens // TILE, turn, 0)

        def head(h, _):
            keys = kf[h]
            part[b, h] = lax.dot_general(
                vt[h], keys, (((0,), (0,)), ((), ())), preferred_element_type=jnp.float32
            )
            mown[b, pl.ds(h, 1), :] = jnp.sum(keys.astype(jnp.float32), axis=0, keepdims=True)
            return 0

        lax.fori_loop(0, heads, head, 0)

    def right_copy(b, n):
        return remote(sr.at[b, n], rr.at[b, n], rr_send.at[b, n], rr_recv.at[b, n], span=(s + 1) % ns)

    def left_copy(b, n):
        return remote(sl.at[b, n], rl.at[b, n], rl_send.at[b, n], rl_recv.at[b, n], span=(s + ns - 1) % ns)

    def term(b, n):
        return part[b, pl.ds(n * chunk, chunk)]

    def sums_start(b):
        @pl.when(s == 0)
        def _():
            for n in range(ns - 1, 0, -1):
                sr[b, n] = term(b, n).astype(jnp.bfloat16)
                right_copy(b, n).start()

        @pl.when(s == ns - 1)
        def _():
            for n in range(ns - 1):
                sl[b, n] = term(b, n).astype(jnp.bfloat16)
                left_copy(b, n).start()

    def sums_middle(b, i):
        to_right, to_left = ns - 1 - i, i

        @pl.when((s > 0) & (s < to_right))
        def _():
            right_copy(b, to_right).wait_recv()
            sr[b, to_right] = (term(b, to_right) + rr[b, to_right].astype(jnp.float32)).astype(jnp.bfloat16)
            right_copy(b, to_right).start()

        @pl.when((s < ns - 1) & (s > to_left))
        def _():
            left_copy(b, to_left).wait_recv()
            sl[b, to_left] = (term(b, to_left) + rl[b, to_left].astype(jnp.float32)).astype(jnp.bfloat16)
            left_copy(b, to_left).start()

    def whole(b, n):
        return full.at[b, pl.ds(n * chunk, chunk)]

    def on_right(b, n):
        return remote(whole(b, n), whole(b, n), ag_sr.at[b, n], ag_recv.at[b, n], span=(s + 1) % ns)

    def on_left(b, n):
        return remote(whole(b, n), whole(b, n), ag_sl.at[b, n], ag_recv.at[b, n], span=(s + ns - 1) % ns)

    def sums_end(b):
        acc[...] = term(b, s)

        @pl.when(s > 0)
        def _():
            right_copy(b, s).wait_recv()
            acc[...] += rr[b, s].astype(jnp.float32)

        @pl.when(s < ns - 1)
        def _():
            left_copy(b, s).wait_recv()
            acc[...] += rl[b, s].astype(jnp.float32)

        full[b, pl.ds(s * chunk, chunk)] = (acc[...] / count).astype(jnp.bfloat16)

        @pl.when(s < ns - 1)
        def _():
            on_right(b, s).start()

        @pl.when(s > 0)
        def _():
            on_left(b, s).start()

    def pass_on(b, d):
        @pl.when(s - d >= 0)
        def _():
            on_right(b, s - d).wait_recv()

            @pl.when(s < ns - 1)
            def _():
                on_right(b, s - d).start()

        @pl.when(s + d <= ns - 1)
        def _():
            on_left(b, s + d).wait_recv()

            @pl.when(s > 0)
            def _():
                on_left(b, s + d).start()

    def mass_copy(d):
        return remote(mown, mrecv.at[d], m_send.at[d], m_recv.at[d], span=(s + d) % ns)

    def ready(b, low, high):
        def turn(i, _):
            at = pl.ds(pl.multiple_of(i * TILE, TILE), TILE)
            qf[b, :, at, :] = jnp.swapaxes(feature_map(qin[b, at]), 0, 1)
            gs[b, :, at, :] = jax.nn.sigmoid(jnp.swapaxes(gin[b, at], 0, 1).astype(jnp.float32))
            return 0

        lax.fori_loop(low, high, turn, 0)

    def read(b):
        def head(h, _):
            row = mown[b, pl.ds(h, 1), :]
            for d in range(1, ns):
                row = row + mrecv[d, b, pl.ds(h, 1), :]
            wide = jnp.broadcast_to(row / count, (size, size))
            high = wide.astype(jnp.bfloat16)
            low = (wide - high.astype(jnp.float32)).astype(jnp.bfloat16)
            top = jnp.concatenate([full[b, h], jnp.zeros((size, size), jnp.bfloat16)], axis=1)
            right = jnp.concatenate([top, jnp.concatenate([high, low], axis=1)], axis=0)
            columns = pl.ds(pl.multiple_of(h * size, size), size)
            for t in range(0, tokens, ROWS):
                f = qf[b, h, t : t + ROWS]
                both = lax.dot_general(
                    jnp.concatenate([f, f], axis=1), right, (((1,), (1,)), ((), ())),
                    preferred_element_type=jnp.float32,
                )
                result = both[:, :size] / (both[:, size:] + 0.001) * count**0.5
                mixed[b, t : t + ROWS, columns] = (result * gs[b, h, t : t + ROWS]).astype(jnp.bfloat16)
            return 0

        lax.fori_loop(0, heads, head, 0)
        copy = pltpu.make_async_copy(mixed.at[b], mixed_hbm.at[b], out_sem.at[b])
        copy.start()
        return copy

    for b in range(batch):
        state(b)
        sums_start(b)
    for d in range(1, ns):
        mass_copy(d).start()
    tiles = tokens // TILE
    for i in range(ns):
        for b in range(batch):
            sums_middle(b, i)
        if i == 1:
            weights_a()
        if i < batch:
            for n in (2, 3):
                loads[n, i].wait()
            ready(i, 0, tiles)
    for b in range(min(ns, batch), batch):
        for n in (2, 3):
            loads[n, b].wait()
        ready(b, 0, tiles)
    for b in range(batch):
        sums_end(b)
    for d in range(1, ns):
        for b in range(batch):
            pass_on(b, d)
    weights_b()
    for d in range(1, ns):
        mass_copy(d).wait_recv()
    stored = [read(b) for b in range(batch)]
    weights_c()

    for copy in stored:
        copy.wait()
    keep_w.wait()
    for copy in sends:
        copy.wait_send()
    for d in range(1, ns):
        mass_copy(d).wait_send()
    for b in range(batch):
        for n in range(ns):

            @pl.when(s < n)
            def _():
                right_copy(b, n).wait_send()

            @pl.when(s > n)
            def _():
                left_copy(b, n).wait_send()

            @pl.when((n <= s) & (s < ns - 1))
            def _():
                on_right(b, n).wait_send()

            @pl.when((n >= s) & (s > 0))
            def _():
                on_left(b, n).wait_send()


def body(queries_in, keys_in, values_in, gate_rows, out_weight):
    batch, tokens, heads, size = queries_in.shape
    depth, width = out_weight.shape
    no, ns = lax.axis_size("outer"), lax.axis_size("span")
    chunk = heads // ns
    bf, f32 = jnp.bfloat16, jnp.float32
    dma = pltpu.SemaphoreType.DMA
    anywhere = pl.BlockSpec(memory_space=pl.ANY)
    copies = max(13, no)
    slots = pltpu.VMEM((batch, ns, chunk, size, size), bf)
    block = pltpu.VMEM((batch, tokens, heads, size), bf)
    mixed, weight = pl.pallas_call(
        functools.partial(kernel, no, ns),
        out_shape=(
            jax.ShapeDtypeStruct((batch, tokens, heads * size), bf),
            jax.ShapeDtypeStruct((no * depth, width), bf),
        ),
        in_specs=[anywhere] * 5,
        out_specs=(anywhere, anywhere),
        scratch_shapes=[
            block, block, block, block,
            pltpu.VMEM((depth, width), bf),
            pltpu.VMEM((heads, tokens, size), bf),
            pltpu.VMEM((heads, tokens, size), bf),
            pltpu.VMEM((batch, heads, tokens, size), bf),
            pltpu.VMEM((batch, heads, tokens, size), f32),
            pltpu.VMEM((batch, heads, size, size), f32),
            pltpu.VMEM((chunk, size, size), f32),
            slots, slots, slots, slots,
            pltpu.VMEM((batch, heads, size, size), bf),
            pltpu.VMEM((batch, heads, size), f32),
            pltpu.VMEM((ns, batch, heads, size), f32),
            pltpu.VMEM((batch, tokens, heads * size), bf),
            dma((4, batch)), dma((2,)), dma((batch,)),
            dma((copies,)), dma((copies,)),
            dma((batch, ns)), dma((batch, ns)), dma((batch, ns)), dma((batch, ns)),
            dma((batch, ns)), dma((batch, ns)), dma((batch, ns)),
            dma((ns,)), dma((ns,)),
        ],
        compiler_params=pltpu.CompilerParams(
            collective_id=0, has_side_effects=True, vmem_limit_bytes=60 * 1024 * 1024
        ),
    )(queries_in, keys_in, values_in, gate_rows, out_weight)
    return jnp.einsum("btw,wv->btv", mixed, weight, preferred_element_type=f32).astype(bf)


def solution(mesh):
    rows = P("outer", "span", None, None)
    in_specs = (rows, rows, rows, rows, P("outer", None))
    out_specs = P("outer", "span", None)
    return jax.shard_map(body, mesh=mesh, in_specs=in_specs, out_specs=out_specs, check_vma=False)
```

time: 143 us -> 89.2 us (0.62)
  Pallas kernels: 0 us -> 75.2 us
  waiting for transfers between devices: 43.7 us -> 0 us
  local copies, waits for them, and re-layouts: 22.5 us -> 0 us
  matrix products: 36.1 us -> 13.8 us
  blocking collectives: 21.1 us -> 0 us
  between operations: 14.9 us -> 0.01 us
  other arithmetic: 3.92 us -> 0 us
    pallas_call x0 -> x1, Pallas kernels: none -> 75.2 us  [body(): pl.pallas_call(functools.partial(kernel, no, ns), out_shape=(jax.ShapeDty...]
    psum x1 -> x0, waiting for transfers between devices: 43.1 us -> none  [body(): state, mass = lax.psum((part_state, part_mass), 'span')]
    unnamed x3 -> x0, local copies, waits for them, and re-layouts: 22.5 us -> none
    dot_general x4 -> x1, matrix products: 36.1 us -> 13.8 us  [body(): jnp.einsum('btw,wv->btv', mixed, weight, preferred_element_type=f32)]
    psum x1 -> x0, blocking collectives: 21.1 us -> none  [body(): state, mass = lax.psum((part_state, part_mass), 'span')]
    reduce_sum x1 -> x0, other arithmetic: 3.91 us -> none  [body(): part_mass = jnp.sum(key_feature.astype(jnp.float32), axis=1)]
  transfers between devices with their start and end apart: 2 -> 0, of which waited for: 1 -> 0; matrix products, arithmetic and copies ran while one was open for 23% -> 0% of each run, Pallas kernels for 0% -> 0%
where the time goes in v1:
time: 89.2 us; the launch traced here: 89 us
  Pallas kernels  75.2 us (84%)
  matrix products  13.8 us (15%)
    pallas_call x1, Pallas kernels, body(): pl.pallas_call(functools.partial(kernel, no, ns), out_shape=(jax.ShapeDty...  75.2 us
    dot_general x1, matrix products, body(): jnp.einsum('btw,wv->btv', mixed, weight, preferred_element_type=f32)  13.8 us

profile of v1, /device:TPU:0, one launch (start us, length us, event | category | flops | bytes accessed | tf_op | source)
XLA Modules:
  0.0 89.0 jit_solution(958406657561992765)
XLA Ops:
  0.0 75.2 %shard_map.55 = (bf16[2,512,2048]{2,1,0:T(8,128)(2,1)}, bf16[2048,2048]{1,0:T(8,128)(2,1)}) custom-call(bf16[2,512,16,128]{3,2,1,0:T(8,128)(2,1)} %q_hbm.1, bf16[2,512,16,128]{3,2,1,0:T(8,128)(2,1)} %k_hbm.1, bf16[2,512,16,128]{3,2,1,0:T(8,128)(2,1)} %v_hbm.1, bf16[2,512,16,128]{3,2,1,0:T(8,128)(2,1)} %g_hbm.1, bf16[256,2048]{1,0:T(8,128)(2,1)} %w_hbm.1), custom_call_target="tpu_custom_call" | custom-call | tf_op jit(solution)/shard_map/pallas_call | solution.py:339
  75.2 13.8 %fusion.2 = bf16[2,512,2048]{2,1,0:T(8,128)(2,1)} fusion(bf16[2,512,2048]{2,1,0:T(8,128)(2,1)} %get-tuple-element.7, bf16[2048,2048]{1,0:T(8,128)(2,1)} %get-tuple-element.8), kind=kOutput, calls=%fused_computation.2 | convolution fusion | flops 8592031744 | bytes 16777216 | tf_op jit(solution)/shard_map/btw,wv->btv/dot_general | solution.py:371
